TPU v7x, 32 devices: a whole 2x2x4 slice. The times are simulated.
32 devices in a mesh: term: 8 (over z, core), sector: 4 (over y, x).
Axes of the slice: x: 2, y: 2, z: 4, core: 2. Of those that a mesh axis runs over, the one named last changes fastest.
Arguments:
- wavefunction: bfloat16 [24, 256, 256], P('sector'), may hold values from -6 to 6
- left_env: bfloat16 [24, 24, 256, 256], P('term', 'sector')
- right_env: bfloat16 [24, 24, 256, 256], P('term', 'sector')
- source: int32 [24, 24], P('term'), may hold values from 0 to 23, as said below
- block_size: int32 [24, 2], P('sector'), may hold values from 32 to 256
Outputs:
- first_product: float32 [24, 256, 256], P('sector', 'term')
- second_product: float32 [24, 256, 256], P('sector', 'term')
Inputs may be any that keep to these rules, and one draw needn't show every extreme that they name: Owner of sector s is s // 6. Among the 3 x 6 entries of source in one device's rows (one index of term) and columns (one index of sector), at most 5 name sectors of any one owner, and some owner is named exactly 5 times.
All inputs are finite; a program needn't handle non-finite values.
Results may differ from a plain program's by a relative error of at most 0.0037.
Values may be sent and summed in bfloat16 or wider, within the bound.
A program may use at most 64 MiB of HBM per device.

v0:
```python
import jax
import jax.numpy as jnp
from jax import lax
from jax.sharding import PartitionSpec as P

epsilon = 1e-06


def block_mask(block_size, width):
    positions = jnp.arange(width, dtype=jnp.int32)
    row_keep = positions[None, :] < block_size[:, 0:1]
    column_keep = positions[None, :] < block_size[:, 1:2]
    return row_keep[:, :, None] & column_keep[:, None, :]


def fetch_blocks(masked, source):
    local_count = masked.shape[0]
    width = masked.shape[1]
    bond_count = source.shape[0]
    my_index = lax.axis_index("sector")
    item_count = bond_count * local_count
    wanted = lax.dynamic_slice_in_dim(source, my_index * local_count, local_count, 1).reshape(
        item_count
    )
    pieces = lax.all_gather(masked, "sector", axis=0, tiled=True)
    piece_count = pieces.shape[0]
    numbers = jnp.arange(piece_count, dtype=jnp.int32)
    onehot = (wanted[:, None] == numbers[None, :]).astype(jnp.bfloat16)
    picked = jnp.dot(
        onehot, pieces.reshape(piece_count, width * width), preferred_element_type=jnp.float32
    )
    return picked.astype(jnp.bfloat16).reshape(bond_count, local_count, width, width)


def apply_operator(vector, left_env, right_env, source, keep):
    masked = jnp.where(keep, vector, jnp.zeros_like(vector))
    picked = fetch_blocks(masked, source)
    half_product = jnp.einsum(
        "bkij,bkjl->bkil", left_env, picked, preferred_element_type=jnp.float32
    ).astype(jnp.bfloat16)
    bond_terms = jnp.einsum(
        "bkil,bkml->bkim", half_product, right_env, preferred_element_type=jnp.float32
    )
    summed = jnp.sum(bond_terms, axis=0)
    return (jnp.where(keep, summed, jnp.zeros_like(summed)), masked)


def body(wavefunction, left_env, right_env, source, block_size):
    width = wavefunction.shape[1]
    keep = block_mask(block_size, width)
    term_count = lax.axis_size("term")
    term_index = lax.axis_index("term")
    row_count = width // term_count
    total_count = lax.axis_size("sector") * wavefunction.shape[0] * width * width
    partial_value, masked = apply_operator(wavefunction, left_env, right_env, source, keep)
    masked_float = masked.astype(jnp.float32)
    whole_sum = lax.psum(partial_value, "term")
    first_product = lax.dynamic_slice_in_dim(whole_sum, term_index * row_count, row_count, 1)
    margin, self_norm = lax.psum(
        (jnp.sum(masked_float * whole_sum), jnp.sum(masked_float * masked_float)), "sector"
    )
    residual = whole_sum - margin / self_norm * masked_float
    spread = lax.psum(jnp.sum(residual * residual), "sector")
    next_vector = (residual * lax.rsqrt(spread / total_count + epsilon)).astype(jnp.bfloat16)
    second_partial, _ = apply_operator(next_vector, left_env, right_env, source, keep)
    second_product = lax.psum_scatter(second_partial, "term", scatter_dimension=1, tiled=True)
    return (first_product, second_product)


def solution(mesh):
    placed = (
        P("sector", None, None),
        P("term", "sector", None, None),
        P("term", "sector", None, None),
        P("term", None),
        P("sector", None),
    )
    return jax.shard_map(
        body,
        mesh=mesh,
        in_specs=placed,
        out_specs=(P("sector", "term", None), P("sector", "term", None)),
        check_vma=False,
    )
```

profile of v0, /device:TPU:0, one launch (start us, length us, event | category | flops | bytes accessed | tf_op | source)
XLA Modules:
  0.0 256.0 jit_solution(13237176541998194756)
XLA Ops:
  7.2 0.0 copy-start
  7.2 0.0 copy-start.2
  7.2 0.0 all-gather.3.cloned.1.call-start
  7.2 0.9 slice_bitcast_fusion.1
  8.1 0.1 iota_compare_fusion.3
  8.2 2.3 and_select_fusion.3
  10.5 0.0 all-gather.3.cloned.1.call-update
  10.5 0.0 all-reduce.3.cloned.1.call-start
  10.6 0.0 copy-done.2
  10.6 0.1 constant_dynamic-slice_fusion.1
  10.7 0.1 eq.8
  10.8 46.5 %all-gather.3.cloned.1.call-done = bf16[24,256,256]{2,1,0:T(8,128)(2,1)} async-done(((bf16[6,256,256]{2,1,0:T(8,128)(2,1)}), bf16[24,256,256]{2,1,0:T(8,128)(2,1)}) %all-gather.3.cloned.1.call-update) | async-done | bytes 3145744 | tf_op jit(solution)/shard_map/all_gather | solution.py:25
  57.3 3.7 %copy.16 = bf16[3,8,256,256]{3,1,2,0:T(8,128)(2,1)S(1)} copy(bf16[3,8,256,256]{3,2,1,0:T(8,128)(2,1)} %bitcast.40) | data formatting | bytes 6291456
  60.9 1.0 convolution_convert_fusion.1
  62.0 0.7 copy.17
  62.7 1.7 slice.11
  64.4 0.0 copy-done
  64.4 0.0 copy-start.1
  64.4 5.0 %and_select_fusion.2 = f32[6,256,256]{2,1,0:T(8,128)} fusion(bf16[3,6,256,256]{3,2,1,0:T(8,128)(2,1)S(1)} %copy-done, bf16[3,6,256,256]{3,2,1,0:T(8,128)(2,1)} %bitcast.43, bf16[3,6,256,256]{3,2,1,0:T(8,128)(2,1)} %param.6, pred[6,256]{1,0:T(8,128)(4,1)S(1)} %get-tuple-element.8, pred[6,256]{1,0:T(8,128)(4,1)S(1)} %get-tuple-element.9), kind=kOutput, calls=%fused_computation.4 | convolution fusion | flops 1209925632 | bytes 8653824 | tf_op jit(solution)/shard_map/bkil,bkml->bkim/dot_general | solution.py:41
  69.4 0.0 all-reduce.3.cloned.1.call-update
  69.4 0.0 all-gather.5.cloned.1.call-start
  69.5 62.0 %all-reduce.3.cloned.1.call-done = f32[6,256,256]{2,1,0:T(8,128)} async-done(((f32[6,256,256]{2,1,0:T(8,128)}), f32[6,256,256]{2,1,0:T(8,128)}) %all-reduce.3.cloned.1.call-update) | async-done | bytes 1572880 | tf_op jit(solution)/shard_map/psum | solution.py:57
  131.5 0.0 copy-done.1
  131.5 2.6 %fusion.25 = (f32[]{:T(128)}, f32[]{:T(128)}) fusion(f32[6,256,256]{2,1,0:T(8,128)} %all-reduce.3.cloned.1.call-done, bf16[6,256,256]{2,1,0:T(8,128)(2,1)S(1)} %copy-done.1, pred[6,256]{1,0:T(8,128)(4,1)S(1)} %get-tuple-element.8, pred[6,256]{1,0:T(8,128)(4,1)S(1)} %get-tuple-element.9), kind=kLoop, calls=%fused_computation.24 | loop fusion | flops 2752510 | bytes 2362376 | tf_op jit(solution)/shard_map/reduce_sum | solution.py:60
  134.1 10.4 %all-reduce = (f32[]{:T(128)}, f32[]{:T(128)}) all-reduce(f32[]{:T(128)} %get-tuple-element.3, f32[]{:T(128)} %get-tuple-element.2), channel_id=1, replica_groups=mesh['term'=8,'sector'=4] {'sector'}, use_global_device_ids=true, to_apply=%region_2.3 | all-reduce | flops 2 | bytes 16 | tf_op jit(solution)/shard_map/psum | solution.py:59
  145.9 2.6 %multiply_reduce_fusion = f32[]{:T(128)} fusion(f32[6,256,256]{2,1,0:T(8,128)} %all-reduce.3.cloned.1.call-done, f32[]{:T(128)S(6)} %div.6, bf16[6,256,256]{2,1,0:T(8,128)(2,1)S(1)} %copy-done.1, pred[6,256]{1,0:T(8,128)(4,1)S(1)} %get-tuple-element.8, pred[6,256]{1,0:T(8,128)(4,1)S(1)} %get-tuple-element.9), kind=kLoop, calls=%fused_computation.27 | loop fusion | flops 2752511 | bytes 2362376 | tf_op jit(solution)/shard_map/reduce_sum | solution.py:63
  148.5 8.6 %psum.31 = f32[]{:T(128)} all-reduce(f32[]{:T(128)} %multiply_reduce_fusion), channel_id=1, replica_groups=mesh['term'=8,'sector'=4] {'sector'}, use_global_device_ids=true, to_apply=%region_6.7 | all-reduce | flops 1 | bytes 8 | tf_op jit(solution)/shard_map/psum | solution.py:63
  157.8 2.8 %and_select_fusion.1 = bf16[6,256,256]{2,1,0:T(8,128)(2,1)} fusion(f32[6,256,256]{2,1,0:T(8,128)} %all-reduce.3.cloned.1.call-done, f32[]{:T(128)S(6)} %rsqrt.3, f32[]{:T(128)S(6)} %div.6, pred[6,256]{1,0:T(8,128)(4,1)S(1)} %get-tuple-element.8, pred[6,256]{1,0:T(8,128)(4,1)S(1)} %get-tuple-element.9, bf16[6,256,256]{2,1,0:T(8,128)(2,1)S(1)} %copy-done.1), kind=kLoop, calls=%fused_computation.3 | loop fusion | flops 3145728 | bytes 3148808 | tf_op jit(solution)/shard_map/jit(_where)/select_n | solution.py:36
  160.6 0.0 all-gather.5.cloned.1.call-update
  160.6 0.2 reduce-scatter.2.cloned.1.call-start
  160.8 42.1 %all-gather.5.cloned.1.call-done = bf16[24,256,256]{2,1,0:T(8,128)(2,1)} async-done(((bf16[6,256,256]{2,1,0:T(8,128)(2,1)}), bf16[24,256,256]{2,1,0:T(8,128)(2,1)}) %all-gather.5.cloned.1.call-update) | async-done | bytes 3145744 | tf_op jit(solution)/shard_map/all_gather | solution.py:25
  203.0 3.7 %copy.18 = bf16[3,8,256,256]{3,1,2,0:T(8,128)(2,1)S(1)} copy(bf16[3,8,256,256]{3,2,1,0:T(8,128)(2,1)} %bitcast.41) | data formatting | bytes 6291456
  206.6 1.0 convolution_convert_fusion
  207.7 0.7 copy.19
  208.4 1.7 slice.12
  210.1 4.9 %and_select_fusion = f32[6,256,256]{2,1,0:T(8,128)} fusion(bf16[3,6,256,256]{3,2,1,0:T(8,128)(2,1)S(1)} %copy-done, bf16[3,6,256,256]{3,2,1,0:T(8,128)(2,1)} %bitcast.42, bf16[3,6,256,256]{3,2,1,0:T(8,128)(2,1)} %param.6, pred[6,256]{1,0:T(8,128)(4,1)S(1)} %get-tuple-element.8, pred[6,256]{1,0:T(8,128)(4,1)S(1)} %get-tuple-element.9), kind=kOutput, calls=%fused_computation.2 | convolution fusion | flops 1209925632 | bytes 8653824 | tf_op jit(solution)/shard_map/bkil,bkml->bkim/dot_general | solution.py:41
  215.0 0.0 reduce-scatter.2.cloned.1.call-update
  215.0 1.6 constant_dynamic-slice_fusion
  216.7 32.8 %reduce-scatter.2.cloned.1.call-done = f32[6,32,256]{2,1,0:T(8,128)} async-done(((f32[6,256,256]{2,1,0:T(8,128)}), f32[6,32,256]{2,1,0:T(8,128)}) %reduce-scatter.2.cloned.1.call-update) | async-done | bytes 196624 | tf_op jit(solution)/shard_map/reduce_scatter | solution.py:66
Async XLA Ops:
  7.2 57.2 %copy-start = (bf16[3,6,256,256]{3,2,1,0:T(8,128)(2,1)S(1)}, bf16[3,6,256,256]{3,2,1,0:T(8,128)(2,1)}, u32[]{:S(2)}) copy-start(bf16[3,6,256,256]{3,2,1,0:T(8,128)(2,1)} %param.7) | copy-start | bytes 7077892
  7.2 3.4 %copy-start.2 = (s32[3,24]{1,0:T(4,128)S(1)}, s32[3,24]{1,0:T(4,128)}, u32[]{:S(2)}) copy-start(s32[3,24]{1,0:T(4,128)} %param.8) | copy-start | bytes 868
  7.2 50.1 %all-gather.3.cloned.1.call-start = ((), (), s32[]{:S(2)}) async-start(), calls=%async_computation.1 | async-start | bytes 3932160 | tf_op jit(solution)/shard_map/all_gather | solution.py:25
  10.5 120.9 %all-reduce.3.cloned.1.call-start = ((), (), s32[]{:S(2)}) async-start(), calls=%async_computation.2 | async-start | bytes 3145728 | tf_op jit(solution)/shard_map/psum | solution.py:57
  64.4 67.1 %copy-start.1 = (bf16[6,256,256]{2,1,0:T(8,128)(2,1)S(1)}, bf16[6,256,256]{2,1,0:T(8,128)(2,1)}, u32[]{:S(2)}) copy-start(bf16[6,256,256]{2,1,0:T(8,128)(2,1)} %param.5) | copy-start | bytes 2359300
  69.4 133.6 %all-gather.5.cloned.1.call-start = ((), (), s32[]{:S(2)}) async-start(), calls=%async_computation.3 | async-start | bytes 3932160 | tf_op jit(solution)/shard_map/all_gather | solution.py:25
  160.6 88.8 %reduce-scatter.2.cloned.1.call-start = ((), (), s32[]{:S(2)}) async-start(), calls=%async_computation.4 | async-start | bytes 1769472 | tf_op jit(solution)/shard_map/reduce_scatter | solution.py:66
Sparse Core Ops, SparseCore 0:
  10.7 46.5 all-gather.2
  69.5 61.8 all-reduce.2
  160.7 42.1 all-gather.4
  215.1 34.2 reduce-scatter.1
where the time goes:
time: 256 us
  waiting for transfers between devices  183 us (71%)
  blocking collectives  19 us (7%)
  between operations  15.9 us (6%)
  local copies, waits for them, and re-layouts  14.8 us (6%)
  matrix products  12 us (5%)
  other arithmetic  10.5 us (4%)
    all_gather x2, waiting for transfers between devices, fetch_blocks(): pieces = lax.all_gather(masked, 'sector', axis=0, tiled=True)  88.6 us
    psum x1, waiting for transfers between devices, body(): whole_sum = lax.psum(partial_value, 'term')  62 us
    reduce_scatter x1, waiting for transfers between devices, body(): lax.psum_scatter(second_partial, 'term', scatter_dimension=1, tiled=True)  32.8 us
    unnamed x12, local copies, waits for them, and re-layouts  12.1 us
    psum x1, blocking collectives, body(): lax.psum((jnp.sum(masked_float * whole_sum), jnp.sum(masked_float * maske...  10.4 us
    dot_general x2, matrix products, apply_operator(): jnp.einsum('bkil,bkml->bkim', half_product, right_env, preferred_element_...  9.96 us
    psum x1, blocking collectives, body(): spread = lax.psum(jnp.sum(residual * residual), 'sector')  8.58 us
    select_n x2, other arithmetic, apply_operator(): masked = jnp.where(keep, vector, jnp.zeros_like(vector))  5.17 us
  transfers between devices with their start and end apart: 4, of which 4 were waited for; matrix products, arithmetic and copies ran while one was open for 1% of the time, Pallas kernels for 0%

commit v1 on v0

--- a/solution.py
+++ b/solution.py
@@ -4,6 +4,17 @@
 from jax.sharding import PartitionSpec as P
 
 epsilon = 1e-06
+
+
+def turned_line(value, name, along):
+    size = lax.axis_size(name)
+    hops = [(i, (i + 1) % size) for i in range(size)]
+    shards = [value]
+    for hop in range(1, size):
+        shards = [lax.ppermute(shards[0], name, hops), *shards]
+    out = jnp.concatenate(shards, axis=along)
+    shift = (lax.axis_index(name) + 1) * shards[-1].shape[along]
+    return jnp.roll(out, shift, axis=along)
 
 
 def block_mask(block_size, width):
@@ -22,7 +33,7 @@
     wanted = lax.dynamic_slice_in_dim(source, my_index * local_count, local_count, 1).reshape(
         item_count
     )
-    pieces = lax.all_gather(masked, "sector", axis=0, tiled=True)
+    pieces = turned_line(masked, "sector", 0)
     piece_count = pieces.shape[0]
     numbers = jnp.arange(piece_count, dtype=jnp.int32)
     onehot = (wanted[:, None] == numbers[None, :]).astype(jnp.bfloat16)

time: 256 us -> 279 us (1.090)
  waiting for transfers between devices: 183 us -> 192 us
  other arithmetic: 10.5 us -> 18.7 us
  starting transfers between devices: 0.34 us -> 8.32 us
    ppermute x0 -> x6, waiting for transfers between devices: none -> 99.6 us  [turned_line(): shards = [lax.ppermute(shards[0], name, hops), *shards]]
    all_gather x2 -> x0, waiting for transfers between devices: 88.6 us -> none  [fetch_blocks(): pieces = lax.all_gather(masked, 'sector', axis=0, tiled=True)]
    concatenate x0 -> x2, other arithmetic: none -> 9.97 us  [turned_line(): return jnp.roll(out, shift, axis=along)]
    ppermute x0 -> x6, starting transfers between devices: none -> 8.24 us  [turned_line(): shards = [lax.ppermute(shards[0], name, hops), *shards]]
    unnamed x12, local copies, waits for them, and re-layouts: 12.1 us -> 9.24 us
  transfers between devices with their start and end apart: 4 -> 8, of which waited for: 4 -> 8; matrix products, arithmetic and copies ran while one was open for 1% -> 1% of each run, Pallas kernels for 0% -> 0%
where the time goes in v1:
time: 279 us
  waiting for transfers between devices  192 us (69%)
  blocking collectives  19 us (7%)
  other arithmetic  18.7 us (7%)
  between operations  16.2 us (6%)
  local copies, waits for them, and re-layouts  12.6 us (5%)
  matrix products  12 us (4%)
  starting transfers between devices  8.32 us (3%)
    ppermute x6, waiting for transfers between devices, turned_line(): shards = [lax.ppermute(shards[0], name, hops), *shards]  99.6 us
    psum x1, waiting for transfers between devices, body(): whole_sum = lax.psum(partial_value, 'term')  62 us
    reduce_scatter x1, waiting for transfers between devices, body(): lax.psum_scatter(second_partial, 'term', scatter_dimension=1, tiled=True)  30.4 us
    psum x1, blocking collectives, body(): lax.psum((jnp.sum(masked_float * whole_sum), jnp.sum(masked_float * maske...  10.4 us
    dot_general x2, matrix products, apply_operator(): jnp.einsum('bkil,bkml->bkim', half_product, right_env, preferred_element_...  9.98 us
    concatenate x2, other arithmetic, turned_line(): return jnp.roll(out, shift, axis=along)  9.97 us
    unnamed x12, local copies, waits for them, and re-layouts  9.24 us
    psum x1, blocking collectives, body(): spread = lax.psum(jnp.sum(residual * residual), 'sector')  8.58 us
  transfers between devices with their start and end apart: 8, of which 8 were waited for; matrix products, arithmetic and copies ran while one was open for 1% of the time, Pallas kernels for 0%

profile of v1, /device:TPU:0, one launch (start us, length us, event | category | flops | bytes accessed | tf_op | source)
XLA Modules:
  0.0 278.9 jit_solution(8079701151401976124)
XLA Ops:
  7.2 0.0 copy-start
  7.2 0.0 all-reduce.3.cloned.1.call-start
  7.2 0.9 slice_bitcast_fusion.1
  8.1 0.1 iota_compare_fusion.3
  8.2 1.5 and_select_fusion.3
  9.6 3.0 %collective-permute-start = (bf16[6,256,256]{2,1,0:T(8,128)(2,1)S(1)}, bf16[6,256,256]{2,1,0:T(8,128)(2,1)S(1)}, u32[]{:S(2)}, u32[]{:S(2)}) collective-permute-start(bf16[6,256,256]{2,1,0:T(8,128)(2,1)S(1)} %and_select_fusion.3), channel_id=1, source_target_pairs={{0,1},{1,2},{2,3},{3,0},{4,5},{5,6},{6,7},{7,4},{8,9},{9,10},{10,1... | collective-permute-start | bytes 2359304 | tf_op jit(solution)/shard_map/ppermute | solution.py:14
  12.6 18.5 %collective-permute-done = bf16[6,256,256]{2,1,0:T(8,128)(2,1)S(1)} collective-permute-done((bf16[6,256,256]{2,1,0:T(8,128)(2,1)S(1)}, bf16[6,256,256]{2,1,0:T(8,128)(2,1)S(1)}, u32[]{:S(2)}, u32[]{:S(2)}) %collective-permute-start) | collective-permute-done | bytes 786464 | tf_op jit(solution)/shard_map/ppermute | solution.py:14
  31.1 0.0 copy-start.2
  31.1 0.9 copy-done.2
  32.0 0.8 collective-permute-start.1
  32.8 18.9 %collective-permute-done.1 = bf16[6,256,256]{2,1,0:T(8,128)(2,1)} collective-permute-done((bf16[6,256,256]{2,1,0:T(8,128)(2,1)S(1)}, bf16[6,256,256]{2,1,0:T(8,128)(2,1)}, u32[]{:S(2)}, u32[]{:S(2)}) %collective-permute-start.1) | collective-permute-done | bytes 786464 | tf_op jit(solution)/shard_map/ppermute | solution.py:14
  51.7 0.0 collective-permute-start.2
  51.7 0.8 constant_dynamic-slice_fusion.1
  52.5 0.1 eq.10
  52.6 18.2 %collective-permute-done.2 = bf16[6,256,256]{2,1,0:T(8,128)(2,1)} collective-permute-done((bf16[6,256,256]{2,1,0:T(8,128)(2,1)}, bf16[6,256,256]{2,1,0:T(8,128)(2,1)}, u32[]{:S(2)}, u32[]{:S(2)}) %collective-permute-start.2) | collective-permute-done | bytes 786464 | tf_op jit(solution)/shard_map/ppermute | solution.py:14
  70.8 5.3 %fusion.10 = bf16[24,256,256]{2,1,0:T(8,128)(2,1)S(1)} fusion(s32[]{:T(128)S(6)} %select_n.40, bf16[6,256,256]{2,1,0:T(8,128)(2,1)} %collective-permute-done.2, bf16[6,256,256]{2,1,0:T(8,128)(2,1)} %collective-permute-done.1, bf16[6,256,256]{2,1,0:T(8,128)(2,1)} %copy-done.2, bf16[6,256,256]{2,1,0:T(8,128)(2,1)S(1)} %and_select_fusion.3), kind=kLoop, calls=%fused_computation.28 | loop fusion | flops 11010048 | bytes 6291460 | tf_op jit(solution)/shard_map/jit(_roll_dynamic)/concatenate | solution.py:17
  76.1 1.8 copy.14
  77.9 1.0 convolution_convert_fusion.1
  79.0 0.7 copy.15
  79.7 1.6 slice.11
  81.3 0.0 copy-done
  81.3 0.0 copy-start.1
  81.3 5.0 %and_select_fusion.2 = f32[6,256,256]{2,1,0:T(8,128)} fusion(bf16[3,6,256,256]{3,2,1,0:T(8,128)(2,1)S(1)} %copy-done, bf16[3,6,256,256]{3,2,1,0:T(8,128)(2,1)} %bitcast.43, bf16[3,6,256,256]{3,2,1,0:T(8,128)(2,1)} %param.8, pred[6,256]{1,0:T(8,128)(4,1)S(1)} %get-tuple-element.9, pred[6,256]{1,0:T(8,128)(4,1)S(1)} %get-tuple-element.10), kind=kOutput, calls=%fused_computation.34 | convolution fusion | flops 1209925632 | bytes 8653824 | tf_op jit(solution)/shard_map/bkil,bkml->bkim/dot_general | solution.py:52
  86.3 0.0 all-reduce.3.cloned.1.call-update
  86.4 0.0 reduce-scatter.2.cloned.1.call-start
  86.4 62.0 %all-reduce.3.cloned.1.call-done = f32[6,256,256]{2,1,0:T(8,128)} async-done(((f32[6,256,256]{2,1,0:T(8,128)}), f32[6,256,256]{2,1,0:T(8,128)}) %all-reduce.3.cloned.1.call-update) | async-done | bytes 1572880 | tf_op jit(solution)/shard_map/psum | solution.py:68
  148.4 0.0 copy-done.1
  148.4 2.6 fusion.39
  151.0 10.4 %all-reduce = (f32[]{:T(128)}, f32[]{:T(128)}) all-reduce(f32[]{:T(128)} %get-tuple-element.4, f32[]{:T(128)} %get-tuple-element.3), channel_id=1, replica_groups=mesh['term'=8,'sector'=4] {'sector'}, use_global_device_ids=true, to_apply=%region_2.4 | all-reduce | flops 2 | bytes 16 | tf_op jit(solution)/shard_map/psum | solution.py:70
  162.8 2.6 multiply_reduce_fusion
  165.5 8.6 %psum.31 = f32[]{:T(128)} all-reduce(f32[]{:T(128)} %multiply_reduce_fusion), channel_id=1, replica_groups=mesh['term'=8,'sector'=4] {'sector'}, use_global_device_ids=true, to_apply=%region_6.8 | all-reduce | flops 1 | bytes 8 | tf_op jit(solution)/shard_map/psum | solution.py:74
  174.7 1.9 and_select_fusion.1
  176.7 1.5 collective-permute-start.3
  178.2 16.2 %collective-permute-done.3 = bf16[6,256,256]{2,1,0:T(8,128)(2,1)S(1)} collective-permute-done((bf16[6,256,256]{2,1,0:T(8,128)(2,1)S(1)}, bf16[6,256,256]{2,1,0:T(8,128)(2,1)S(1)}, u32[]{:S(2)}, u32[]{:S(2)}) %collective-permute-start.3) | collective-permute-done | bytes 786464 | tf_op jit(solution)/shard_map/ppermute | solution.py:14
  194.4 1.5 collective-permute-start.4
  195.9 16.2 %collective-permute-done.4 = bf16[6,256,256]{2,1,0:T(8,128)(2,1)S(1)} collective-permute-done((bf16[6,256,256]{2,1,0:T(8,128)(2,1)S(1)}, bf16[6,256,256]{2,1,0:T(8,128)(2,1)S(1)}, u32[]{:S(2)}, u32[]{:S(2)}) %collective-permute-start.4) | collective-permute-done | bytes 786464 | tf_op jit(solution)/shard_map/ppermute | solution.py:14
  212.1 1.5 collective-permute-start.5
  213.6 11.5 %collective-permute-done.5 = bf16[6,256,256]{2,1,0:T(8,128)(2,1)S(1)} collective-permute-done((bf16[6,256,256]{2,1,0:T(8,128)(2,1)S(1)}, bf16[6,256,256]{2,1,0:T(8,128)(2,1)S(1)}, u32[]{:S(2)}, u32[]{:S(2)}) %collective-permute-start.5) | collective-permute-done | bytes 786464 | tf_op jit(solution)/shard_map/ppermute | solution.py:14
  225.1 4.7 %fusion.3 = bf16[24,256,256]{2,1,0:T(8,128)(2,1)S(1)} fusion(s32[]{:T(128)S(6)} %select_n.40, bf16[6,256,256]{2,1,0:T(8,128)(2,1)S(1)} %collective-permute-done.5, bf16[6,256,256]{2,1,0:T(8,128)(2,1)S(1)} %collective-permute-done.4, bf16[6,256,256]{2,1,0:T(8,128)(2,1)S(1)} %collective-permute-done.3, bf16[6,256,256]{2,1,0:T(8,128)(2,1)S(1)} %and_select_fusion.1), kind=kLoop, calls=%fused_computation.21 | loop fusion | flops 11010048 | bytes 6291460 | tf_op jit(solution)/shard_map/jit(_roll_dynamic)/concatenate | solution.py:17
  229.7 1.8 copy.16
  231.6 1.0 convolution_convert_fusion
  232.6 0.7 copy.17
  233.3 1.6 slice.12
  235.0 5.0 %and_select_fusion = f32[6,256,256]{2,1,0:T(8,128)} fusion(bf16[3,6,256,256]{3,2,1,0:T(8,128)(2,1)S(1)} %copy-done, bf16[3,6,256,256]{3,2,1,0:T(8,128)(2,1)} %bitcast.42, bf16[3,6,256,256]{3,2,1,0:T(8,128)(2,1)} %param.8, pred[6,256]{1,0:T(8,128)(4,1)S(1)} %get-tuple-element.9, pred[6,256]{1,0:T(8,128)(4,1)S(1)} %get-tuple-element.10), kind=kOutput, calls=%fused_computation.32 | convolution fusion | flops 1209925632 | bytes 8653824 | tf_op jit(solution)/shard_map/bkil,bkml->bkim/dot_general | solution.py:52
  239.9 0.0 reduce-scatter.2.cloned.1.call-update
  239.9 1.6 constant_dynamic-slice_fusion
  241.6 30.4 %reduce-scatter.2.cloned.1.call-done = f32[6,32,256]{2,1,0:T(8,128)} async-done(((f32[6,256,256]{2,1,0:T(8,128)}), f32[6,32,256]{2,1,0:T(8,128)}) %reduce-scatter.2.cloned.1.call-update) | async-done | bytes 196624 | tf_op jit(solution)/shard_map/reduce_scatter | solution.py:77
Async XLA Ops:
  7.2 74.2 %copy-start = (bf16[3,6,256,256]{3,2,1,0:T(8,128)(2,1)S(1)}, bf16[3,6,256,256]{3,2,1,0:T(8,128)(2,1)}, u32[]{:S(2)}) copy-start(bf16[3,6,256,256]{3,2,1,0:T(8,128)(2,1)} %param.9) | copy-start | bytes 7077892
  7.2 141.2 %all-reduce.3.cloned.1.call-start = ((), (), s32[]{:S(2)}) async-start(), calls=%async_computation.1 | async-start | bytes 3145728 | tf_op jit(solution)/shard_map/psum | solution.py:68
  9.6 21.5 %collective-permute-start = (bf16[6,256,256]{2,1,0:T(8,128)(2,1)S(1)}, bf16[6,256,256]{2,1,0:T(8,128)(2,1)S(1)}, u32[]{:S(2)}, u32[]{:S(2)}) collective-permute-start(bf16[6,256,256]{2,1,0:T(8,128)(2,1)S(1)} %and_select_fusion.3), channel_id=1, source_target_pairs={{0,1},{1,2},{2,3},{3,0},{4,5},{5,6},{6,7},{7,4},{8,9},{9,10},{10,1... | collective-permute-start | bytes 2359304 | tf_op jit(solution)/shard_map/ppermute | solution.py:14
  31.1 0.9 copy-start.2
  32.0 19.7 %collective-permute-start.1 = (bf16[6,256,256]{2,1,0:T(8,128)(2,1)S(1)}, bf16[6,256,256]{2,1,0:T(8,128)(2,1)}, u32[]{:S(2)}, u32[]{:S(2)}) collective-permute-start(bf16[6,256,256]{2,1,0:T(8,128)(2,1)S(1)} %collective-permute-done), channel_id=1, source_target_pairs={{0,1},{1,2},{2,3},{3,0},{4,5},{5,6},{6,7},{7,4},{8,9},{9,10},{10,1... | collective-permute-start | bytes 2359304 | tf_op jit(solution)/shard_map/ppermute | solution.py:14
  51.7 19.1 %collective-permute-start.2 = (bf16[6,256,256]{2,1,0:T(8,128)(2,1)}, bf16[6,256,256]{2,1,0:T(8,128)(2,1)}, u32[]{:S(2)}, u32[]{:S(2)}) collective-permute-start(bf16[6,256,256]{2,1,0:T(8,128)(2,1)} %collective-permute-done.1), channel_id=1, source_target_pairs={{0,1},{1,2},{2,3},{3,0},{4,5},{5,6},{6,7},{7,4},{8,9},{9,10},{10,1... | collective-permute-start | bytes 2359304 | tf_op jit(solution)/shard_map/ppermute | solution.py:14
  81.3 67.1 %copy-start.1 = (bf16[6,256,256]{2,1,0:T(8,128)(2,1)S(1)}, bf16[6,256,256]{2,1,0:T(8,128)(2,1)}, u32[]{:S(2)}) copy-start(bf16[6,256,256]{2,1,0:T(8,128)(2,1)} %param.7) | copy-start | bytes 2359300
  86.4 185.6 %reduce-scatter.2.cloned.1.call-start = ((), (), s32[]{:S(2)}) async-start(), calls=%async_computation.2 | async-start | bytes 1769472 | tf_op jit(solution)/shard_map/reduce_scatter | solution.py:77
  176.7 17.8 %collective-permute-start.3 = (bf16[6,256,256]{2,1,0:T(8,128)(2,1)S(1)}, bf16[6,256,256]{2,1,0:T(8,128)(2,1)S(1)}, u32[]{:S(2)}, u32[]{:S(2)}) collective-permute-start(bf16[6,256,256]{2,1,0:T(8,128)(2,1)S(1)} %and_select_fusion.1), channel_id=1, source_target_pairs={{0,1},{1,2},{2,3},{3,0},{4,5},{5,6},{6,7},{7,4},{8,9},{9,10},{10,1... | collective-permute-start | bytes 2359304 | tf_op jit(solution)/shard_map/ppermute | solution.py:14
  194.4 17.7 %collective-permute-start.4 = (bf16[6,256,256]{2,1,0:T(8,128)(2,1)S(1)}, bf16[6,256,256]{2,1,0:T(8,128)(2,1)S(1)}, u32[]{:S(2)}, u32[]{:S(2)}) collective-permute-start(bf16[6,256,256]{2,1,0:T(8,128)(2,1)S(1)} %collective-permute-done.3), channel_id=1, source_target_pairs={{0,1},{1,2},{2,3},{3,0},{4,5},{5,6},{6,7},{7,4},{8,9},{9,10},{10,1... | collective-permute-start | bytes 2359304 | tf_op jit(solution)/shard_map/ppermute | solution.py:14
  212.1 12.9 %collective-permute-start.5 = (bf16[6,256,256]{2,1,0:T(8,128)(2,1)S(1)}, bf16[6,256,256]{2,1,0:T(8,128)(2,1)S(1)}, u32[]{:S(2)}, u32[]{:S(2)}) collective-permute-start(bf16[6,256,256]{2,1,0:T(8,128)(2,1)S(1)} %collective-permute-done.4), channel_id=1, source_target_pairs={{0,1},{1,2},{2,3},{3,0},{4,5},{5,6},{6,7},{7,4},{8,9},{9,10},{10,1... | collective-permute-start | bytes 2359304 | tf_op jit(solution)/shard_map/ppermute | solution.py:14
Sparse Core Ops, SparseCore 0:
  86.5 61.8 all-reduce.2
  240.1 31.9 reduce-scatter.1
